TPU v7x, 32 devices: a whole 2x2x4 slice. The times are simulated.
32 devices in a mesh: dp: 8 (over y, x, core), mp: 4 (over z).
Axes of the slice: x: 2, y: 2, z: 4, core: 2. Of those that a mesh axis runs over, the one named last changes fastest.
Arguments:
- feature_ids: int32 [8, 2048, 8], P('dp'), may hold values from 0 to 4095
- tables: bfloat16 [8, 4096, 128], P('dp'), may hold values from -5 to 5
- table_of_feature: int32 [8], replicated, may hold values from 0 to 7, each once
- cross_down: bfloat16 [2, 1024, 512], P(None, 'mp'), may hold values from -0.1875 to 0.1875
- cross_up: bfloat16 [2, 1024, 512], P(None, 'mp'), may hold values from -0.125 to 0.125
- cross_bias: float32 [2, 1024], P(None, 'mp'), may hold values from -3 to 3
- tower_weight: bfloat16 [1024, 2048], P('dp', 'mp'), may hold values from -0.1875 to 0.1875
- tower_bias: float32 [2048], P('mp'), may hold values from -3 to 3
Outputs:
- hidden: bfloat16 [2048, 2048], P('dp', 'mp')
Inputs may be any that keep to these rules, and one draw needn't show every extreme that they name: `feature_ids`: each id indexes a row of its own table. `table_of_feature`: each table serves exactly one feature.
All inputs are finite; a program needn't handle non-finite values.
Results may differ from a plain program's by a relative error of at most 0.015.
Values may be sent and summed in bfloat16 or wider, within the bound.
A program may use at most 64 MiB of HBM per device.

v0:
```python
import jax
import jax.numpy as jnp
from jax import lax
from jax.sharding import PartitionSpec as P


def body(
    feature_ids,
    tables,
    table_of_feature,
    cross_down,
    cross_up,
    cross_bias,
    tower_weight,
    tower_bias,
):
    groups = lax.axis_size("dp")
    members = lax.axis_size("mp")
    member = lax.axis_index("mp")
    table_count, batch_size, hot_count = feature_ids.shape
    row_count = batch_size // (groups * members)
    shaped = feature_ids[0].reshape(groups, members, row_count, hot_count)
    own_ids = lax.dynamic_index_in_dim(shaped, member, 1, keepdims=False).reshape(
        groups * row_count, hot_count
    )
    summed = jnp.zeros((groups * row_count, tables.shape[2]), jnp.float32)
    for hot_index in range(hot_count):
        summed = summed + jnp.take(tables[0], own_ids[:, hot_index], axis=0).astype(jnp.float32)
    columns = [summed.astype(jnp.bfloat16)]
    pooled = jnp.stack(columns, axis=1)
    regrouped = lax.all_to_all(pooled, "dp", split_axis=0, concat_axis=1, tiled=True)
    ordered = jnp.take(regrouped, table_of_feature, axis=1)
    by_width = lax.all_to_all(ordered, "mp", split_axis=1, concat_axis=0, tiled=True)
    group_rows = by_width.shape[0]
    embedded = by_width.reshape(group_rows, -1)
    embedded_wide = embedded.astype(jnp.float32)
    crossed = embedded
    layer_total = cross_down.shape[0]
    for layer_index in range(layer_total):
        partial_value = jnp.dot(
            crossed, cross_down[layer_index], preferred_element_type=jnp.float32
        )
        projected = lax.psum(partial_value.astype(jnp.bfloat16), "mp")
        lifted = lax.dot_general(
            projected,
            cross_up[layer_index],
            (((1,), (1,)), ((), ())),
            preferred_element_type=jnp.float32,
        )
        crossed = (
            embedded_wide * (lifted + cross_bias[layer_index]) + crossed.astype(jnp.float32)
        ).astype(jnp.bfloat16)
    full_rows = lax.all_gather(crossed, "mp", axis=1, tiled=True)
    pre_act = jnp.dot(
        full_rows,
        lax.all_gather(tower_weight, "dp", axis=0, tiled=True),
        preferred_element_type=jnp.float32,
    )
    return jax.nn.relu(pre_act + tower_bias).astype(jnp.bfloat16)


def solution(mesh):
    return jax.shard_map(
        body,
        mesh=mesh,
        in_specs=(
            P("dp", None, None),
            P("dp", None, None),
            P(),
            P(None, "mp", None),
            P(None, "mp", None),
            P(None, "mp"),
            P("dp", "mp"),
            P("mp"),
        ),
        out_specs=P("dp", "mp"),
        check_vma=False,
    )
```

profile of v0, /device:TPU:0, one launch (start us, length us, event | category | flops | bytes accessed | tf_op | source)
XLA Modules:
  0.0 143.6 jit_solution(9518459660529289800)
XLA Ops:
  7.4 0.0 copy-start
  7.4 1.0 reshape_squeeze.3
  8.4 0.1 dynamic-slice_reduce_fusion
  8.5 0.1 reshape.19
  8.8 0.0 copy-done
  8.8 1.3 gather_fusion.2
  10.2 1.3 gather_fusion.3
  11.5 1.3 gather_fusion.4
  12.9 1.3 gather_fusion.5
  14.2 1.3 gather_fusion.6
  15.6 1.3 gather_fusion.7
  17.0 1.3 gather_fusion.8
  18.3 1.3 gather_fusion.1
  19.7 0.8 fusion.16
  20.5 0.5 broadcast.59
  21.0 0.7 reduce.4
  21.7 0.7 reshape.125
  22.3 0.0 copy-start.5
  22.3 5.3 %all-to-all-start = ((bf16[8,2,4096]{2,1,0:T(2,128)(2,1)}), bf16[8,2,4096]{2,1,0:T(2,128)(2,1)S(1)}, u32[]{:S(2)}, u32[]{:S(2)}) async-start(bf16[8,2,4096]{2,1,0:T(2,128)(2,1)} %reshape.125), calls=%async_computation | async-start | bytes 262144 | tf_op jit(solution)/shard_map/all_to_all | solution.py:31
  27.7 0.0 all-reduce.3.cloned.1.call-start
  27.7 0.0 copy-done.5
  27.8 5.4 %all-to-all-done = bf16[8,2,4096]{2,1,0:T(2,128)(2,1)S(1)} async-done(((bf16[8,2,4096]{2,1,0:T(2,128)(2,1)}), bf16[8,2,4096]{2,1,0:T(2,128)(2,1)S(1)}, u32[]{:S(2)}, u32[]{:S(2)}) %all-to-all-start) | async-done | bytes 131104 | tf_op jit(solution)/shard_map/all_to_all | solution.py:31
  33.2 0.1 reshape.126
  33.3 0.0 copy-start.1
  33.3 0.6 gather_fusion
  33.9 0.1 select_bitcast_fusion
  34.0 10.6 %all_to_all.33 = bf16[64,8,128]{2,0,1:T(8,128)(2,1)S(1)} all-to-all(bf16[64,8,128]{2,0,1:T(8,128)(2,1)S(1)} %select_bitcast_fusion), channel_id=1, replica_groups=mesh['dp'=8,'mp'=4] {'mp'}, dimensions={1} | all-to-all | bytes 262144 | tf_op jit(solution)/shard_map/all_to_all | solution.py:33
  44.6 0.1 copy.13
  44.8 0.0 copy-start.3
  44.8 0.0 copy-done.1
  44.8 0.9 convolution_convert_fusion.1
  45.7 0.0 copy-start.2
  45.7 0.0 all-reduce.3.cloned.1.call-update
  45.8 0.0 all-reduce.5.cloned.1.call-start
  45.8 0.6 copy-done.2
  46.4 32.4 %all-reduce.3.cloned.1.call-done = bf16[256,512]{1,0:T(8,128)(2,1)} async-done(((bf16[256,512]{1,0:T(8,128)(2,1)}), bf16[256,512]{1,0:T(8,128)(2,1)}) %all-reduce.3.cloned.1.call-update) | async-done | bytes 262160 | tf_op jit(solution)/shard_map/psum | solution.py:43
  78.8 0.0 copy-done.3
  78.8 1.2 fusion.6
  80.0 0.9 convolution_convert_fusion
  80.9 0.0 all-reduce.5.cloned.1.call-update
  81.0 0.0 all-gather.2.cloned.1.call-start
  81.0 0.5 all-gather.2.cloned.1.call-update
  81.5 35.1 %all-reduce.5.cloned.1.call-done = bf16[256,512]{1,0:T(8,128)(2,1)} async-done(((bf16[256,512]{1,0:T(8,128)(2,1)}), bf16[256,512]{1,0:T(8,128)(2,1)}) %all-reduce.5.cloned.1.call-update) | async-done | bytes 262160 | tf_op jit(solution)/shard_map/psum | solution.py:43
  116.6 1.2 fusion.7
  117.8 0.0 copy-start.4
  117.8 16.0 %all_gather.6 = bf16[256,1024]{1,0:T(8,128)(2,1)S(1)} all-gather(bf16[256,256]{1,0:T(8,128)(2,1)S(1)} %fusion.7), channel_id=1, replica_groups=mesh['dp'=8,'mp'=4] {'mp'}, dimensions={1}, use_global_device_ids=true | all-gather | bytes 655360 | tf_op jit(solution)/shard_map/all_gather | solution.py:53
  133.8 0.0 copy-done.4
  133.8 2.4 %fusion.1 = bf16[256,512]{1,0:T(8,128)(2,1)} fusion(bf16[256,1024]{1,0:T(8,128)(2,1)S(1)} %all_gather.6, bf16[1024,512]{1,0:T(8,128)(2,1)} %all-gather.2.cloned.1.call-done, f32[512]{0:T(512)S(1)} %copy-done.4), kind=kOutput, calls=%fused_computation.11 | convolution fusion | flops 268828672 | bytes 1837056 | tf_op jit(solution)/shard_map/dot_general | solution.py:54
  (27 shorter events, 0.2 us)
Async XLA Ops:
  7.4 1.4 %copy-start = (bf16[1,4096,128]{2,1,0:T(8,128)(2,1)S(1)}, bf16[1,4096,128]{2,1,0:T(8,128)(2,1)}, u32[]{:S(2)}) copy-start(bf16[1,4096,128]{2,1,0:T(8,128)(2,1)} %param.11) | copy-start | bytes 3145732
  22.3 5.4 %copy-start.5 = (s32[8]{0:T(128)S(1)}, s32[8]{0:T(128)}, u32[]{:S(2)}) copy-start(s32[8]{0:T(128)} %param.12) | copy-start | bytes 100
  22.3 10.8 %all-to-all-start = ((bf16[8,2,4096]{2,1,0:T(2,128)(2,1)}), bf16[8,2,4096]{2,1,0:T(2,128)(2,1)S(1)}, u32[]{:S(2)}, u32[]{:S(2)}) async-start(bf16[8,2,4096]{2,1,0:T(2,128)(2,1)} %reshape.125), calls=%async_computation | async-start | bytes 262144 | tf_op jit(solution)/shard_map/all_to_all | solution.py:31
  27.7 51.1 %all-reduce.3.cloned.1.call-start = ((), (), s32[]{:S(2)}) async-start(), calls=%async_computation.2 | async-start | bytes 524288 | tf_op jit(solution)/shard_map/psum | solution.py:43
  33.3 11.5 %copy-start.1 = (bf16[2,256,512]{2,1,0:T(8,128)(2,1)S(1)}, bf16[2,256,512]{2,1,0:T(8,128)(2,1)}, u32[]{:S(2)}) copy-start(bf16[2,256,512]{2,1,0:T(8,128)(2,1)} %param.13) | copy-start | bytes 1572868
  44.8 34.0 %copy-start.3 = (bf16[2,256,512]{2,1,0:T(8,128)(2,1)S(1)}, bf16[2,256,512]{2,1,0:T(8,128)(2,1)}, u32[]{:S(2)}) copy-start(bf16[2,256,512]{2,1,0:T(8,128)(2,1)} %param.14) | copy-start | bytes 1572868
  45.7 0.7 copy-start.2
  45.8 70.8 %all-reduce.5.cloned.1.call-start = ((), (), s32[]{:S(2)}) async-start(), calls=%async_computation.3 | async-start | bytes 524288 | tf_op jit(solution)/shard_map/psum | solution.py:43
  81.0 52.8 %all-gather.2.cloned.1.call-start = ((), (), s32[]{:S(2)}) async-start(), calls=%async_computation.4 | async-start | bytes 1179648 | tf_op jit(solution)/shard_map/all_gather | solution.py:56
  117.8 16.0 %copy-start.4 = (f32[512]{0:T(512)S(1)}, f32[512]{0:T(512)}, u32[]{:S(2)}) copy-start(f32[512]{0:T(512)} %param.17) | copy-start | bytes 6148
Sparse Core Ops, SparseCore 0:
  45.9 32.8 all-reduce.2
  81.1 35.4 all-reduce.4
Sparse Core Ops, SparseCore 1:
  83.3 23.1 all-gather.1
where the time goes:
time: 144 us
  waiting for transfers between devices  73.4 us (51%)
  blocking collectives  26.6 us (18%)
  between operations  15.2 us (11%)
  local copies, waits for them, and re-layouts  14.7 us (10%)
  matrix products  6.65 us (5%)
  starting transfers between devices  5.45 us (4%)
  other arithmetic  1.66 us (1%)
    psum x2, waiting for transfers between devices, body(): projected = lax.psum(partial_value.astype(jnp.bfloat16), 'mp')  67.4 us
    all_gather x1, blocking collectives, body(): full_rows = lax.all_gather(crossed, 'mp', axis=1, tiled=True)  16 us
    gather x8, local copies, waits for them, and re-layouts, body(): jnp.take(tables[0], own_ids[:, hot_index], axis=0).astype(jnp.float32)  10.7 us
    all_to_all x1, blocking collectives, body(): lax.all_to_all(ordered, 'mp', split_axis=1, concat_axis=0, tiled=True)  10.6 us
    all_to_all x1, waiting for transfers between devices, body(): lax.all_to_all(pooled, 'dp', split_axis=0, concat_axis=1, tiled=True)  5.4 us
    all_to_all x1, starting transfers between devices, body(): lax.all_to_all(pooled, 'dp', split_axis=0, concat_axis=1, tiled=True)  5.33 us
  transfers between devices with their start and end apart: 4, of which 3 were waited for; matrix products, arithmetic and copies ran while one was open for 1% of the time, Pallas kernels for 0%

commit v1 on v0

--- a/solution.py
+++ b/solution.py
@@ -30,7 +30,9 @@
     pooled = jnp.stack(columns, axis=1)
     regrouped = lax.all_to_all(pooled, "dp", split_axis=0, concat_axis=1, tiled=True)
     ordered = jnp.take(regrouped, table_of_feature, axis=1)
-    by_width = lax.all_to_all(ordered, "mp", split_axis=1, concat_axis=0, tiled=True)
+    cells = jnp.split(ordered, lax.axis_size("mp"), axis=1)
+    incoming = lax.all_to_all(jnp.stack(cells), "mp", 0, 0)
+    by_width = jnp.concatenate(incoming, axis=0)
     group_rows = by_width.shape[0]
     embedded = by_width.reshape(group_rows, -1)
     embedded_wide = embedded.astype(jnp.float32)

time: 144 us -> 144 us (level)
  no operation moved by 1% of the time
where the time goes in v1:
time: 144 us
  waiting for transfers between devices  73.3 us (51%)
  blocking collectives  26.7 us (19%)
  between operations  15.2 us (11%)
  local copies, waits for them, and re-layouts  14.7 us (10%)
  matrix products  6.66 us (5%)
  starting transfers between devices  5.45 us (4%)
  other arithmetic  1.68 us (1%)
    psum x2, waiting for transfers between devices, body(): projected = lax.psum(partial_value.astype(jnp.bfloat16), 'mp')  67.4 us
    all_gather x1, blocking collectives, body(): full_rows = lax.all_gather(crossed, 'mp', axis=1, tiled=True)  16 us
    all_to_all x1, blocking collectives, body(): incoming = lax.all_to_all(jnp.stack(cells), 'mp', 0, 0)  10.8 us
    gather x8, local copies, waits for them, and re-layouts, body(): jnp.take(tables[0], own_ids[:, hot_index], axis=0).astype(jnp.float32)  10.7 us
    all_to_all x1, waiting for transfers between devices, body(): lax.all_to_all(pooled, 'dp', split_axis=0, concat_axis=1, tiled=True)  5.4 us
    all_to_all x1, starting transfers between devices, body(): lax.all_to_all(pooled, 'dp', split_axis=0, concat_axis=1, tiled=True)  5.33 us
  transfers between devices with their start and end apart: 4, of which 3 were waited for; matrix products, arithmetic and copies ran while one was open for 1% of the time, Pallas kernels for 0%

profile of v1, /device:TPU:0, one launch (start us, length us, event | category | flops | bytes accessed | tf_op | source)
XLA Modules:
  0.0 143.8 jit_solution(15382437378141541168)
XLA Ops:
  7.4 0.0 copy-start
  7.4 1.0 reshape_squeeze.3
  8.4 0.1 dynamic-slice_reduce_fusion
  8.5 0.1 reshape.15
  8.8 0.0 copy-done
  8.8 1.3 gather_fusion.2
  10.2 1.3 gather_fusion.3
  11.5 1.3 gather_fusion.4
  12.9 1.3 gather_fusion.5
  14.2 1.3 gather_fusion.6
  15.6 1.3 gather_fusion.7
  17.0 1.3 gather_fusion.8
  18.3 1.3 gather_fusion.1
  19.7 0.8 fusion.16
  20.5 0.5 broadcast.59
  21.0 0.7 reduce.4
  21.7 0.7 reshape.120
  22.3 0.0 copy-start.5
  22.3 5.3 %all-to-all-start = ((bf16[8,2,4096]{2,1,0:T(2,128)(2,1)}), bf16[8,2,4096]{2,1,0:T(2,128)(2,1)S(1)}, u32[]{:S(2)}, u32[]{:S(2)}) async-start(bf16[8,2,4096]{2,1,0:T(2,128)(2,1)} %reshape.120), calls=%async_computation | async-start | bytes 262144 | tf_op jit(solution)/shard_map/all_to_all | solution.py:31
  27.7 0.0 all-reduce.3.cloned.1.call-start
  27.7 0.0 copy-done.5
  27.8 5.4 %all-to-all-done = bf16[8,2,4096]{2,1,0:T(2,128)(2,1)S(1)} async-done(((bf16[8,2,4096]{2,1,0:T(2,128)(2,1)}), bf16[8,2,4096]{2,1,0:T(2,128)(2,1)S(1)}, u32[]{:S(2)}, u32[]{:S(2)}) %all-to-all-start) | async-done | bytes 131104 | tf_op jit(solution)/shard_map/all_to_all | solution.py:31
  33.2 0.1 reshape.121
  33.3 0.6 gather_fusion
  33.9 0.1 select_bitcast_fusion
  34.0 0.0 copy-start.1
  34.1 10.8 %all_to_all.23 = bf16[4,64,2,128]{3,1,2,0:T(8,128)(2,1)S(1)} all-to-all(bf16[4,64,2,128]{3,1,2,0:T(8,128)(2,1)S(1)} %pad_maximum_fusion), channel_id=1, replica_groups=mesh['dp'=8,'mp'=4] {'mp'}, dimensions={0} | all-to-all | bytes 262144 | tf_op jit(solution)/shard_map/all_to_all | solution.py:34
  44.8 0.1 copy.13
  45.0 0.0 copy-start.3
  45.0 0.0 copy-done.1
  45.0 0.9 convolution_convert_fusion.1
  45.9 0.0 copy-start.2
  45.9 0.0 all-reduce.3.cloned.1.call-update
  46.0 0.0 all-reduce.5.cloned.1.call-start
  46.0 0.6 copy-done.2
  46.6 32.3 %all-reduce.3.cloned.1.call-done = bf16[256,512]{1,0:T(8,128)(2,1)} async-done(((bf16[256,512]{1,0:T(8,128)(2,1)}), bf16[256,512]{1,0:T(8,128)(2,1)}) %all-reduce.3.cloned.1.call-update) | async-done | bytes 262160 | tf_op jit(solution)/shard_map/psum | solution.py:45
  79.0 0.0 copy-done.3
  79.0 1.2 fusion.6
  80.2 0.9 convolution_convert_fusion
  81.1 0.0 all-reduce.5.cloned.1.call-update
  81.1 0.0 all-gather.2.cloned.1.call-start
  81.2 0.5 all-gather.2.cloned.1.call-update
  81.7 35.0 %all-reduce.5.cloned.1.call-done = bf16[256,512]{1,0:T(8,128)(2,1)} async-done(((bf16[256,512]{1,0:T(8,128)(2,1)}), bf16[256,512]{1,0:T(8,128)(2,1)}) %all-reduce.5.cloned.1.call-update) | async-done | bytes 262160 | tf_op jit(solution)/shard_map/psum | solution.py:45
  116.8 1.2 fusion.7
  118.0 0.0 copy-start.4
  118.0 16.0 %all_gather.6 = bf16[256,1024]{1,0:T(8,128)(2,1)S(1)} all-gather(bf16[256,256]{1,0:T(8,128)(2,1)S(1)} %fusion.7), channel_id=1, replica_groups=mesh['dp'=8,'mp'=4] {'mp'}, dimensions={1}, use_global_device_ids=true | all-gather | bytes 655360 | tf_op jit(solution)/shard_map/all_gather | solution.py:55
  133.9 0.0 copy-done.4
  134.0 2.4 %fusion.1 = bf16[256,512]{1,0:T(8,128)(2,1)} fusion(bf16[256,1024]{1,0:T(8,128)(2,1)S(1)} %all_gather.6, bf16[1024,512]{1,0:T(8,128)(2,1)} %all-gather.2.cloned.1.call-done, f32[512]{0:T(512)S(1)} %copy-done.4), kind=kOutput, calls=%fused_computation.11 | convolution fusion | flops 268828672 | bytes 1837056 | tf_op jit(solution)/shard_map/dot_general | solution.py:56
  (29 shorter events, 0.2 us)
Async XLA Ops:
  7.4 1.4 %copy-start = (bf16[1,4096,128]{2,1,0:T(8,128)(2,1)S(1)}, bf16[1,4096,128]{2,1,0:T(8,128)(2,1)}, u32[]{:S(2)}) copy-start(bf16[1,4096,128]{2,1,0:T(8,128)(2,1)} %param.11) | copy-start | bytes 3145732
  22.3 5.4 %copy-start.5 = (s32[8]{0:T(128)S(1)}, s32[8]{0:T(128)}, u32[]{:S(2)}) copy-start(s32[8]{0:T(128)} %param.12) | copy-start | bytes 100
  22.3 10.8 %all-to-all-start = ((bf16[8,2,4096]{2,1,0:T(2,128)(2,1)}), bf16[8,2,4096]{2,1,0:T(2,128)(2,1)S(1)}, u32[]{:S(2)}, u32[]{:S(2)}) async-start(bf16[8,2,4096]{2,1,0:T(2,128)(2,1)} %reshape.120), calls=%async_computation | async-start | bytes 262144 | tf_op jit(solution)/shard_map/all_to_all | solution.py:31
  27.7 51.3 %all-reduce.3.cloned.1.call-start = ((), (), s32[]{:S(2)}) async-start(), calls=%async_computation.2 | async-start | bytes 524288 | tf_op jit(solution)/shard_map/psum | solution.py:45
  34.0 11.0 %copy-start.1 = (bf16[2,256,512]{2,1,0:T(8,128)(2,1)S(1)}, bf16[2,256,512]{2,1,0:T(8,128)(2,1)}, u32[]{:S(2)}) copy-start(bf16[2,256,512]{2,1,0:T(8,128)(2,1)} %param.13) | copy-start | bytes 1572868
  45.0 34.0 %copy-start.3 = (bf16[2,256,512]{2,1,0:T(8,128)(2,1)S(1)}, bf16[2,256,512]{2,1,0:T(8,128)(2,1)}, u32[]{:S(2)}) copy-start(bf16[2,256,512]{2,1,0:T(8,128)(2,1)} %param.14) | copy-start | bytes 1572868
  45.9 0.7 copy-start.2
  46.0 70.8 %all-reduce.5.cloned.1.call-start = ((), (), s32[]{:S(2)}) async-start(), calls=%async_computation.3 | async-start | bytes 524288 | tf_op jit(solution)/shard_map/psum | solution.py:45
  81.1 52.8 %all-gather.2.cloned.1.call-start = ((), (), s32[]{:S(2)}) async-start(), calls=%async_computation.4 | async-start | bytes 1179648 | tf_op jit(solution)/shard_map/all_gather | solution.py:58
  118.0 16.0 %copy-start.4 = (f32[512]{0:T(512)S(1)}, f32[512]{0:T(512)}, u32[]{:S(2)}) copy-start(f32[512]{0:T(512)} %param.17) | copy-start | bytes 6148
Sparse Core Ops, SparseCore 0:
  46.1 32.8 all-reduce.2
  81.3 35.4 all-reduce.4
Sparse Core Ops, SparseCore 1:
  83.5 23.1 all-gather.1
